TPU v7x, 32 devices: a whole 2x2x4 slice. The times are simulated.
32 devices in a mesh: grp: 4 (over x, core), dp: 8 (over z, y).
Axes of the slice: x: 2, y: 2, z: 4, core: 2. Of those that a mesh axis runs over, the one named last changes fastest.
Arguments:
- gradients: bfloat16 [4, 8, 16384, 128], P('grp', 'dp'), may hold values from -48 to 48
- block_len: int32 [16], replicated, may hold values from 1 to 524288, 2097152 in all
- amax_history: float32 [4, 16], replicated, may hold values from 20 to 200
Outputs:
- mean_grad: bfloat16 [16384, 128], P('dp')
- block_amax: bfloat16 [16], replicated
Inputs may be any that keep to these rules, and one draw needn't show every extreme that they name: `block_len`: every tensor has at least one entry; the lengths sum to 2097152.
All inputs are finite; a program needn't handle non-finite values.
Results may differ from a plain program's by a relative error of at most 0.018.
Values may be sent and summed in bfloat16 or wider, within the bound.
A program may use at most 64 MiB of HBM per device.

v0:
```python
import jax
import jax.numpy as jnp
from jax import lax
from jax.sharding import PartitionSpec as P

SATURATE = 448.0


def body(gradients, block_len, amax_history):
    dp_count = lax.axis_size("dp")
    grp_count = lax.axis_size("grp")
    bucket = gradients[0, 0]
    all_rows = bucket.shape[0]
    shard_rows = all_rows // dp_count
    devices = dp_count * grp_count
    summed = lax.psum_scatter(
        bucket.astype(jnp.float32).astype(jnp.bfloat16), "dp", scatter_dimension=0, tiled=True
    ).astype(jnp.float32)
    offset = lax.axis_index("dp") * shard_rows
    block_ends = jnp.cumsum(block_len)
    position = (offset + jnp.arange(shard_rows, dtype=jnp.int32))[:, None] * 128 + jnp.arange(
        128, dtype=jnp.int32
    )[None, :]
    block = jnp.sum((position[:, :, None] >= block_ends[None, None, :]).astype(jnp.int32), axis=-1)
    in_block = block[:, :, None] == jnp.arange(block_len.shape[0], dtype=jnp.int32)[None, None, :]
    scales = SATURATE / jnp.maximum(jnp.max(amax_history, axis=0), 1.0)
    scale_elem = jnp.sum(jnp.where(in_block, scales[None, None, :], jnp.float32(0.0)), axis=-1)
    local_max = jnp.max(
        jnp.where(in_block, jnp.abs(summed)[:, :, None], jnp.float32(0.0)), axis=(0, 1)
    ).astype(jnp.bfloat16)
    quantized = jnp.clip(summed * scale_elem, -SATURATE, SATURATE).astype(jnp.bfloat16)
    group_max = lax.pmax(local_max, "dp")
    gathered, group_maxima = (
        lax.all_gather(quantized[None], "grp", axis=0, tiled=True),
        lax.all_gather(group_max[None], "grp", axis=0, tiled=True),
    )
    block_amax = jnp.max(group_maxima, axis=0)
    accumulated = jnp.sum(gathered, axis=0, dtype=jnp.float32)
    mean_grad = (accumulated / scale_elem / devices).astype(jnp.bfloat16)
    return (mean_grad, block_amax)


def solution(mesh):
    placed = (P("grp", "dp", None, None), P(), P())
    return jax.shard_map(
        body, mesh=mesh, in_specs=placed, out_specs=(P("dp", None), P()), check_vma=False
    )
```

profile of v0, /device:TPU:0, one launch (start us, length us, event | category | flops | bytes accessed | tf_op | source)
XLA Modules:
  0.0 156.8 jit_solution(3263560330524715165)
XLA Ops:
  7.2 0.0 copy-start.1
  7.2 0.0 copy-start
  7.2 0.0 reduce-scatter.2.cloned.1.call-start
  7.2 0.7 reduce-scatter.2.cloned.1.call-update
  7.9 0.0 all-gather.4.cloned.1.call-start
  8.0 0.0 copy-done.1
  8.0 0.1 copy.8
  8.1 0.1 reduce.1
  8.2 0.0 copy-done
  8.3 0.3 iota_add_fusion
  8.6 11.6 %convert_reduce_fusion = s32[2048,128]{1,0:T(8,128)S(1)} fusion(s32[2048,128]{1,0:T(8,128)S(1)} %iota_add_fusion, s32[16]{0:T(128)S(1)} %reduce.1), kind=kLoop, calls=%fused_computation.3 | loop fusion | flops 12320768 | bytes 2097216 | tf_op jit(solution)/shard_map/reduce_sum | solution.py:24
  20.2 82.5 %reduce-scatter.2.cloned.1.call-done = bf16[2048,128]{1,0:T(8,128)(2,1)} async-done(((bf16[16384,128]{1,0:T(8,128)(2,1)}), bf16[2048,128]{1,0:T(8,128)(2,1)}) %reduce-scatter.2.cloned.1.call-update) | async-done | bytes 524304 | tf_op jit(solution)/shard_map/reduce_scatter | solution.py:16
  102.7 1.1 convert_abs_fusion
  103.9 15.4 %select_reduce_fusion = (bf16[16]{0:T(256)(128)(2,1)S(1)}, f32[2048,128]{1,0:T(8,128)S(1)}) fusion(bf16[2048,128]{1,0:T(8,128)(2,1)S(1)} %convert_abs_fusion, s32[2048,128]{1,0:T(8,128)S(1)} %convert_reduce_fusion, f32[16]{0:T(128)S(1)} %maximum_divide_fusion), kind=kLoop, calls=%fused_computation | loop fusion | flops 20709360 | bytes 2621536 | tf_op jit(solution)/shard_map/reduce_max | solution.py:28
  119.3 2.0 %fusion.1 = bf16[2048,128]{1,0:T(8,128)(2,1)} fusion(f32[2048,128]{1,0:T(8,128)S(1)} %get-tuple-element.3, bf16[2048,128]{1,0:T(8,128)(2,1)} %reduce-scatter.2.cloned.1.call-done), kind=kLoop, calls=%fused_computation.8 | loop fusion | flops 1048576 | bytes 2097152 | tf_op jit(solution)/shard_map/convert_element_type | solution.py:31
  121.3 0.0 all-gather.4.cloned.1.call-update
  121.3 20.1 %pmax.7 = bf16[1,16]{1,0:T(2,128)(2,1)S(1)} all-reduce(bf16[1,16]{1,0:T(2,128)(2,1)S(1)} %bitcast.10), channel_id=1, replica_groups=mesh['grp'=4,'dp'=8] {'dp'}, use_global_device_ids=true, to_apply=%region_7.8 | all-reduce | flops 16 | bytes 64 | tf_op jit(solution)/shard_map/pmax | solution.py:32
  141.4 5.0 %all-gather.1 = bf16[4,1,16]{2,1,0:T(2,128)(2,1)S(1)} all-gather(bf16[1,1,16]{2,1,0:T(2,128)(2,1)S(1)} %bitcast.12), channel_id=1, replica_groups=mesh['grp'=4,'dp'=8] {'grp'}, dimensions={0}, use_global_device_ids=true | all-gather | bytes 160 | tf_op jit(solution)/shard_map/all_gather | solution.py:35
  146.4 0.5 reduce_max.29
  147.0 0.0 all-gather.4.cloned.1.call-done
  147.0 2.0 %convert_reduce_fusion.1 = f32[2048,128]{1,0:T(8,128)S(1)} fusion(bf16[4,2048,128]{2,1,0:T(8,128)(2,1)} %bitcast.9), kind=kLoop, calls=%fused_computation.4 | loop fusion | flops 1835008 | bytes 3145728 | tf_op jit(solution)/shard_map/reduce_sum | solution.py:38
  149.0 0.9 multiply_convert_fusion
  (4 shorter events, 0.1 us)
Async XLA Ops:
  7.2 0.8 copy-start.1
  7.2 1.0 copy-start
  7.2 95.5 %reduce-scatter.2.cloned.1.call-start = ((), (), s32[]{:S(2)}) async-start(), calls=%async_computation.1 | async-start | bytes 4718592 | tf_op jit(solution)/shard_map/reduce_scatter | solution.py:16
  7.9 139.0 %all-gather.4.cloned.1.call-start = ((), (), s32[]{:S(2)}) async-start(), calls=%async_computation.2 | async-start | bytes 2621440 | tf_op jit(solution)/shard_map/all_gather | solution.py:34
Sparse Core Ops, SparseCore 0:
  11.6 91.0 reduce-scatter.1
  121.4 22.1 all-gather.3
where the time goes:
time: 157 us
  waiting for transfers between devices  83.2 us (53%)
  other arithmetic  34.2 us (22%)
  blocking collectives  25.1 us (16%)
  between operations  14.1 us (9%)
    reduce_scatter x1, waiting for transfers between devices, body(): lax.psum_scatter(bucket.astype(jnp.float32).astype(jnp.bfloat16), 'dp', s...  82.5 us
    pmax x1, blocking collectives, body(): group_max = lax.pmax(local_max, 'dp')  20.1 us
    reduce_max x1, other arithmetic, body(): jnp.max(jnp.where(in_block, jnp.abs(summed)[:, :, None], jnp.float32(0.0)...  15.4 us
    reduce_sum x1, other arithmetic, body(): jnp.sum((position[:, :, None] >= block_ends[None, None, :]).astype(jnp.in...  11.6 us
    all_gather x1, blocking collectives, body(): lax.all_gather(group_max[None], 'grp', axis=0, tiled=True)  5.05 us
  transfers between devices with their start and end apart: 2, of which 1 were waited for; matrix products, arithmetic and copies ran while one was open for 8% of the time, Pallas kernels for 0%

commit v1 on v0

v1 whole, which is shorter than its diff:
```python
import functools

import jax
import jax.numpy as jnp
from jax import lax
from jax.experimental import pallas as pl
from jax.experimental.pallas import tpu as pltpu
from jax.sharding import PartitionSpec as P

SATURATE = 448.0
CHUNKS = 8
CORES = 2
MESH = pl.DeviceIdType.MESH


def y_extent(dp):
    y = 1
    while (2 * y) * (2 * y) <= dp:
        y *= 2
    return y


def kernel(
    cfg, len_ref, hist_ref, grad, out, amax_out,
    own, ybuf, part, zbuf, q, cbuf, xbuf, scale_buf, svec, acc, msg, dpmax, grpmsg, grpmax,
    own_sem, y_send, y_recv, z_send, z_recv, c_send, c_recv, x_send, x_recv,
    o_send, o_recv, dm_send, dm_recv, gm_send, gm_recv,
):
    dp, grp, Y, Z, X, K, H, piece = cfg
    blocks = len_ref.shape[0]
    hist = hist_ref.shape[0]
    d = lax.axis_index("dp")
    g = lax.axis_index("grp")
    z, y = d // Y, d % Y
    x, core = g // CORES, g % CORES
    sibling = x * CORES + (1 - core)
    lines = CORES * H
    base = d * (K * lines)

    def copy(src, dst, send, recv, target):
        return pltpu.make_async_remote_copy(
            src_ref=src, dst_ref=dst, send_sem=send, recv_sem=recv,
            device_id=target, device_id_type=MESH,
        )

    def own_copy(k):
        return pltpu.make_async_copy(grad.at[:, y, k], own.at[k], own_sem.at[k])

    def y_copy(k, j):
        peer = (y + j) % Y
        return copy(grad.at[:, peer, k], ybuf.at[k, j - 1], y_send.at[k, j - 1],
                    y_recv.at[k, j - 1], {"dp": z * Y + peer})

    def z_copy(k, j):
        peer = (z + j) % Z
        return copy(part.at[k, j - 1], zbuf.at[k, j - 1], z_send.at[k, j - 1],
                    z_recv.at[k, j - 1], {"dp": peer * Y + y})

    def c_copy(k):
        return copy(q.at[k, 1 - core], cbuf.at[k], c_send.at[k], c_recv.at[k],
                    {"grp": sibling})

    def x_copy(k, j):
        peer = (x + j) % X
        return copy(xbuf.at[k, x], xbuf.at[k, x], x_send.at[k, j - 1], x_recv.at[k, j - 1],
                    {"grp": peer * CORES + core})

    def x_arrival(k, j):
        peer = (x + X - j) % X
        return copy(xbuf.at[k, peer], xbuf.at[k, peer], x_send.at[k, j - 1],
                    x_recv.at[k, j - 1], {"grp": peer * CORES + core})

    def o_copy(k):
        return copy(out.at[k, core], out.at[k, core], o_send.at[k], o_recv.at[k],
                    {"grp": sibling})

    def o_arrival(k):
        return copy(out.at[k, 1 - core], out.at[k, 1 - core], o_send.at[k], o_recv.at[k],
                    {"grp": sibling})

    def dm_copy(j):
        return copy(msg, dpmax.at[j - 1], dm_send.at[j - 1], dm_recv.at[j - 1],
                    {"dp": (d + j) % dp})

    def gm_copy(j):
        return copy(grpmsg, grpmax.at[j - 1], gm_send.at[j - 1], gm_recv.at[j - 1],
                    {"grp": (g + j) % grp})

    barrier = pltpu.get_barrier_semaphore()
    for j in range(1, dp):
        pl.semaphore_signal(barrier, inc=1, device_id={"dp": (d + j) % dp}, device_id_type=MESH)
    for j in range(1, grp):
        pl.semaphore_signal(barrier, inc=1, device_id={"grp": (g + j) % grp}, device_id_type=MESH)

    def load(k, carry):
        own_copy(k).start()
        return carry

    lax.fori_loop(0, K, load, 0)
    ends = []
    total = jnp.int32(0)
    for c in range(blocks):
        total = total + len_ref[c]
        ends.append(total)
        top = jnp.full((8, 128), hist_ref[0, c], jnp.float32)
        for h in range(1, hist):
            top = jnp.maximum(top, jnp.full((8, 128), hist_ref[h, c], jnp.float32))
        svec[c] = SATURATE / jnp.maximum(top, 1.0)
    acc[...] = jnp.zeros(acc.shape, jnp.float32)
    pl.semaphore_wait(barrier, dp - 1 + grp - 1)

    def send_y(k, carry):
        for j in range(1, Y):
            y_copy(k, j).start()
        return carry

    lax.fori_loop(0, K, send_y, 0)

    def stage_z(k):
        own_copy(k).wait()
        for j in range(1, Y):
            y_copy(k, j).wait_recv()
        for j in range(1, Z):
            peer = (z + j) % Z
            value = own[k, peer].astype(jnp.float32)
            for i in range(Y - 1):
                value = value + ybuf[k, i, peer].astype(jnp.float32)
            part[k, j - 1] = value.astype(jnp.bfloat16)
            z_copy(k, j).start()

    def stage_q(k):
        for j in range(1, Z):
            z_copy(k, j).wait_recv()
        for half in range(CORES):
            def step(i, tops):
                rows = pl.ds(pl.multiple_of(i * piece, piece), piece)
                value = own[k, z, half, rows].astype(jnp.float32)
                for a in range(Y - 1):
                    value = value + ybuf[k, a, z, half, rows].astype(jnp.float32)
                for a in range(Z - 1):
                    value = value + zbuf[k, a, half, rows].astype(jnp.float32)
                value = value.reshape(piece // 8, 8, 128)
                shape = value.shape
                first = (base + k * lines + half * H + i * piece) * 128
                place = (
                    lax.broadcasted_iota(jnp.int32, shape, 0) * 1024
                    + lax.broadcasted_iota(jnp.int32, shape, 1) * 128
                    + lax.broadcasted_iota(jnp.int32, shape, 2)
                ) + first
                size = jnp.abs(value)
                scale = jnp.broadcast_to(svec[0][None], shape)
                below = place < ends[0]
                new = [jnp.maximum(tops[0], jnp.max(jnp.where(below, size, 0.0), axis=0))]
                for c in range(1, blocks):
                    after = place >= ends[c - 1]
                    scale = jnp.where(after, svec[c][None], scale)
                    inside = after & (place < ends[c])
                    new.append(jnp.maximum(tops[c], jnp.max(jnp.where(inside, size, 0.0), axis=0)))
                scale_buf[k, half, rows] = scale.reshape(piece, 128)
                quant = jnp.clip(value * scale, -SATURATE, SATURATE)
                q[k, half, rows] = quant.reshape(piece, 128).astype(jnp.bfloat16)
                return tuple(new)

            tops = lax.fori_loop(0, H // piece, step, tuple(acc[c] for c in range(blocks)))
            for c in range(blocks):
                acc[c] = tops[c]
        c_copy(k).start()

    def stage_max():
        top = jnp.max(acc[...], axis=1)
        top = jnp.max(top, axis=1, keepdims=True)
        lane = lax.broadcasted_iota(jnp.int32, (blocks, 128), 1)
        row = lax.broadcasted_iota(jnp.int32, (blocks, 128), 0)
        flat = jnp.max(jnp.where(lane == row, top, 0.0), axis=0, keepdims=True)
        msg[...] = jnp.broadcast_to(flat, msg.shape)
        for j in range(1, dp):
            dm_copy(j).start()

    def stage_x(k):
        c_copy(k).wait_recv()
        both = q[k, core].astype(jnp.float32) + cbuf[k].astype(jnp.float32)
        xbuf[k, x] = both.astype(jnp.bfloat16)
        for j in range(1, X):
            x_copy(k, j).start()

    def stage_out(k):
        for j in range(1, X):
            x_arrival(k, j).wait_recv()
        value = xbuf[k, 0].astype(jnp.float32)
        for a in range(1, X):
            value = value + xbuf[k, a].astype(jnp.float32)
        mean = value / scale_buf[k, core] / (dp * grp)
        out[k, core] = mean.astype(jnp.bfloat16)
        o_copy(k).start()

    stages = ((stage_z, 0), (stage_q, 2), (stage_x, 3), (stage_out, 4))

    def tick(t, carry):
        for stage, delay in stages:
            @pl.when((t >= delay) & (t < K + delay))
            def _(stage=stage, delay=delay):
                stage(t - delay)

            if stage is stage_q:
                @pl.when(t == K - 1 + delay)
                def _():
                    stage_max()
        return carry

    lax.fori_loop(0, K + 4, tick, 0)

    for j in range(1, dp):
        dm_copy(j).wait_recv()
    top = msg[...]
    for j in range(1, dp):
        top = jnp.maximum(top, dpmax[j - 1])
    grpmsg[...] = top
    for j in range(1, grp):
        gm_copy(j).start()
    for j in range(1, grp):
        gm_copy(j).wait_recv()
    for j in range(1, grp):
        top = jnp.maximum(top, grpmax[j - 1])
    amax_out[...] = top

    def finish(k, carry):
        for j in range(1, Y):
            y_copy(k, j).wait_send()
        for j in range(1, Z):
            z_copy(k, j).wait_send()
        c_copy(k).wait_send()
        for j in range(1, X):
            x_copy(k, j).wait_send()
        o_copy(k).wait_send()
        o_arrival(k).wait_recv()
        return carry

    lax.fori_loop(0, K, finish, 0)
    for j in range(1, dp):
        dm_copy(j).wait_send()
    for j in range(1, grp):
        gm_copy(j).wait_send()


def body(gradients, block_len, amax_history):
    dp = lax.axis_size("dp")
    grp = lax.axis_size("grp")
    rows, lanes = gradients.shape[2:]
    Y = y_extent(dp)
    Z = dp // Y
    X = grp // CORES
    K = CHUNKS
    H = rows // dp // K // CORES
    piece = min(32, H)
    blocks = block_len.shape[0]
    cfg = (dp, grp, Y, Z, X, K, H, piece)
    bf, f32 = jnp.bfloat16, jnp.float32
    sem = pltpu.SemaphoreType.DMA
    tile = (CORES, H, lanes)
    scratch = [
        pltpu.VMEM((K, Z) + tile, bf),
        pltpu.VMEM((K, Y - 1, Z) + tile, bf),
        pltpu.VMEM((K, Z - 1) + tile, bf),
        pltpu.VMEM((K, Z - 1) + tile, bf),
        pltpu.VMEM((K,) + tile, bf),
        pltpu.VMEM((K, H, lanes), bf),
        pltpu.VMEM((K, X, H, lanes), bf),
        pltpu.VMEM((K,) + tile, f32),
        pltpu.VMEM((blocks, 8, lanes), f32),
        pltpu.VMEM((blocks, 8, lanes), f32),
        pltpu.VMEM((8, lanes), f32),
        pltpu.VMEM((dp - 1, 8, lanes), f32),
        pltpu.VMEM((8, lanes), f32),
        pltpu.VMEM((grp - 1, 8, lanes), f32),
        sem((K,)),
        sem((K, Y - 1)), sem((K, Y - 1)),
        sem((K, Z - 1)), sem((K, Z - 1)),
        sem((K,)), sem((K,)),
        sem((K, X - 1)), sem((K, X - 1)),
        sem((K,)), sem((K,)),
        sem((dp - 1,)), sem((dp - 1,)),
        sem((grp - 1,)), sem((grp - 1,)),
    ]
    mean, top = pl.pallas_call(
        functools.partial(kernel, cfg),
        out_shape=(
            jax.ShapeDtypeStruct((K,) + tile, bf),
            jax.ShapeDtypeStruct((8, lanes), f32),
        ),
        in_specs=[
            pl.BlockSpec(memory_space=pltpu.SMEM),
            pl.BlockSpec(memory_space=pltpu.SMEM),
            pl.BlockSpec(memory_space=pl.ANY),
        ],
        out_specs=(
            pl.BlockSpec(memory_space=pltpu.VMEM),
            pl.BlockSpec(memory_space=pltpu.VMEM),
        ),
        scratch_shapes=scratch,
        compiler_params=pltpu.CompilerParams(collective_id=0, has_side_effects=True),
    )(block_len, amax_history, gradients.reshape((Z, Y, K) + tile))
    return mean.reshape(rows // dp, lanes), top[0, :blocks].astype(bf)


def solution(mesh):
    placed = (P("grp", "dp", None, None), P(), P())
    return jax.shard_map(
        body, mesh=mesh, in_specs=placed, out_specs=(P("dp", None), P()), check_vma=False
    )
```

time: 157 us -> 73.8 us (0.47)
  waiting for transfers between devices: 83.2 us -> 0 us
  Pallas kernels: 0 us -> 69.9 us
  other arithmetic: 34.2 us -> 0.68 us
  blocking collectives: 25.1 us -> 0 us
  between operations: 14.1 us -> 0.64 us
  local copies, waits for them, and re-layouts: 0.09 us -> 2.38 us
    reduce_scatter x1 -> x0, waiting for transfers between devices: 82.5 us -> none  [body(): lax.psum_scatter(bucket.astype(jnp.float32).astype(jnp.bfloat16), 'dp', s...]
    pallas_call x0 -> x1, Pallas kernels: none -> 69.9 us  [body(): pl.pallas_call(functools.partial(kernel, cfg), out_shape=(jax.ShapeDtypeS...]
    pmax x1 -> x0, blocking collectives: 20.1 us -> none  [body(): group_max = lax.pmax(local_max, 'dp')]
    reduce_max x3 -> x0, other arithmetic: 16 us -> none  [the longest x1 15.4 us: body(): jnp.max(jnp.where(in_block, jnp.abs(summed)[:, :, None], jnp.float32(0.0)...]
    reduce_sum x2 -> x0, other arithmetic: 13.6 us -> none  [the longest x1 11.6 us: body(): jnp.sum((position[:, :, None] >= block_ends[None, None, :]).astype(jnp.in...]
    all_gather x1 -> x0, blocking collectives: 5.05 us -> none  [body(): lax.all_gather(group_max[None], 'grp', axis=0, tiled=True)]
    convert_element_type x2 -> x0, other arithmetic: 2.92 us -> none  [the longest x1 1.97 us: body(): jnp.clip(summed * scale_elem, -SATURATE, SATURATE).astype(jnp.bfloat16)]
    unnamed x4 -> x1, local copies, waits for them, and re-layouts: 0.01 us -> 1.87 us
  transfers between devices with their start and end apart: 2 -> 0, of which waited for: 1 -> 0; matrix products, arithmetic and copies ran while one was open for 8% -> 0% of each run, Pallas kernels for 0% -> 0%
where the time goes in v1:
time: 73.8 us; the launch traced here: 73.6 us
  Pallas kernels  69.9 us (95%)
  local copies, waits for them, and re-layouts  2.38 us (3%)
    pallas_call x1, Pallas kernels, body(): pl.pallas_call(functools.partial(kernel, cfg), out_shape=(jax.ShapeDtypeS...  69.9 us
    unnamed x1, local copies, waits for them, and re-layouts  1.87 us

profile of v1, /device:TPU:0, one launch (start us, length us, event | category | flops | bytes accessed | tf_op | source)
XLA Modules:
  0.0 73.6 jit_solution(13491959988104484767)
XLA Ops:
  0.6 69.9 %shard_map.50 = (bf16[8,2,128,128]{3,2,1,0:T(8,128)(2,1)}, f32[8,128]{1,0:T(8,128)}) custom-call(s32[16]{0:T(128)} %len_ref.1, f32[4,16]{1,0:T(4,128)} %hist_ref.1, bf16[4,2,8,2,128,128]{5,4,3,2,1,0:T(8,128)(2,1)} %bitcast.4), custom_call_target="tpu_custom_call" | custom-call | tf_op jit(solution)/shard_map/pallas_call | solution.py:284
  70.6 0.7 convert.3
  71.2 0.5 slice_bitcast_fusion
  71.8 1.9 %copy.6 = bf16[2048,128]{1,0:T(8,128)(2,1)} copy(bf16[2048,128]{1,0:T(8,128)(2,1)} %bitcast.5) | data formatting | bytes 1048576

commit v2 on v1

v2 whole, which is shorter than its diff:
```python
import functools

import jax
import jax.numpy as jnp
from jax import lax
from jax.experimental import pallas as pl
from jax.experimental.pallas import tpu as pltpu
from jax.sharding import PartitionSpec as P

SATURATE = 448.0
CHUNKS = 16
DELAYS = (0, 3, 5)
MESH = pl.DeviceIdType.MESH


def y_extent(dp):
    y = 1
    while (2 * y) * (2 * y) <= dp:
        y *= 2
    return y


def kernel(
    cfg, len_ref, hist_ref, grad, out, amax_out,
    own, ybuf, part, zbuf, qbuf, scale_buf, svec, acc, msg, dpmax, grpmsg, grpmax,
    own_sem, y_send, y_recv, z_send, z_recv, q_send, q_recv,
    dm_send, dm_recv, gm_send, gm_recv,
):
    dp, grp, Y, Z, K, lines, piece = cfg
    blocks = len_ref.shape[0]
    hist = hist_ref.shape[0]
    d = lax.axis_index("dp")
    g = lax.axis_index("grp")
    z, y = d // Y, d % Y
    base = d * (K * lines)

    def copy(src, dst, send, recv, target):
        return pltpu.make_async_remote_copy(
            src_ref=src, dst_ref=dst, send_sem=send, recv_sem=recv,
            device_id=target, device_id_type=MESH,
        )

    def own_copy(k):
        return pltpu.make_async_copy(grad.at[:, y, k], own.at[k], own_sem.at[k])

    def y_copy(k, j):
        peer = (y + j) % Y
        return copy(grad.at[:, peer, k], ybuf.at[k, j - 1], y_send.at[k, j - 1],
                    y_recv.at[k, j - 1], {"dp": z * Y + peer})

    def z_copy(k, j):
        peer = (z + j) % Z
        return copy(part.at[k, j - 1], zbuf.at[k, j - 1], z_send.at[k, j - 1],
                    z_recv.at[k, j - 1], {"dp": peer * Y + y})

    def q_copy(k, j):
        return copy(qbuf.at[k, g], qbuf.at[k, g], q_send.at[k, j - 1], q_recv.at[k, j - 1],
                    {"grp": (g + j) % grp})

    def q_arrival(k, j):
        peer = (g + grp - j) % grp
        return copy(qbuf.at[k, peer], qbuf.at[k, peer], q_send.at[k, j - 1],
                    q_recv.at[k, j - 1], {"grp": peer})

    def dm_copy(j):
        return copy(msg, dpmax.at[j - 1], dm_send.at[j - 1], dm_recv.at[j - 1],
                    {"dp": (d + j) % dp})

    def gm_copy(j):
        return copy(grpmsg, grpmax.at[j - 1], gm_send.at[j - 1], gm_recv.at[j - 1],
                    {"grp": (g + j) % grp})

    barrier = pltpu.get_barrier_semaphore()
    for j in range(1, dp):
        pl.semaphore_signal(barrier, inc=1, device_id={"dp": (d + j) % dp}, device_id_type=MESH)
    for j in range(1, grp):
        pl.semaphore_signal(barrier, inc=1, device_id={"grp": (g + j) % grp}, device_id_type=MESH)

    def load(k, carry):
        own_copy(k).start()
        return carry

    lax.fori_loop(0, K, load, 0)
    ends = []
    total = jnp.int32(0)
    for c in range(blocks):
        total = total + len_ref[c]
        ends.append(total)
        top = jnp.full((8, 128), hist_ref[0, c], jnp.float32)
        for h in range(1, hist):
            top = jnp.maximum(top, jnp.full((8, 128), hist_ref[h, c], jnp.float32))
        svec[c] = SATURATE / jnp.maximum(top, 1.0)
    acc[...] = jnp.zeros(acc.shape, jnp.float32)
    pl.semaphore_wait(barrier, dp - 1 + grp - 1)

    def send_y(k, carry):
        for j in range(1, Y):
            y_copy(k, j).start()
        return carry

    lax.fori_loop(0, K, send_y, 0)

    def stage_z(k):
        own_copy(k).wait()
        for j in range(1, Y):
            y_copy(k, j).wait_recv()
        for j in range(1, Z):
            peer = (z + j) % Z
            value = own[k, peer].astype(jnp.float32)
            for i in range(Y - 1):
                value = value + ybuf[k, i, peer].astype(jnp.float32)
            part[k, j - 1] = value.astype(jnp.bfloat16)
            z_copy(k, j).start()

    def stage_q(k):
        for j in range(1, Z):
            z_copy(k, j).wait_recv()
        def step(i, tops):
            rows = pl.ds(pl.multiple_of(i * piece, piece), piece)
            value = own[k, z, rows].astype(jnp.float32)
            for a in range(Y - 1):
                value = value + ybuf[k, a, z, rows].astype(jnp.float32)
            for a in range(Z - 1):
                value = value + zbuf[k, a, rows].astype(jnp.float32)
            value = value.reshape(piece // 8, 8, 128)
            shape = value.shape
            first = (base + k * lines + i * piece) * 128
            place = (
                lax.broadcasted_iota(jnp.int32, shape, 0) * 1024
                + lax.broadcasted_iota(jnp.int32, shape, 1) * 128
                + lax.broadcasted_iota(jnp.int32, shape, 2)
            ) + first
            size = jnp.abs(value)
            scale = jnp.broadcast_to(svec[0][None], shape)
            below = place < ends[0]
            new = [jnp.maximum(tops[0], jnp.max(jnp.where(below, size, 0.0), axis=0))]
            for c in range(1, blocks):
                after = place >= ends[c - 1]
                scale = jnp.where(after, svec[c][None], scale)
                inside = after & (place < ends[c])
                new.append(jnp.maximum(tops[c], jnp.max(jnp.where(inside, size, 0.0), axis=0)))
            scale_buf[k, rows] = scale.reshape(piece, 128)
            quant = jnp.clip(value * scale, -SATURATE, SATURATE)
            qbuf[k, g, rows] = quant.reshape(piece, 128).astype(jnp.bfloat16)
            return tuple(new)

        tops = lax.fori_loop(0, lines // piece, step, tuple(acc[c] for c in range(blocks)))
        for c in range(blocks):
            acc[c] = tops[c]
        for j in range(1, grp):
            q_copy(k, j).start()

    def stage_max():
        top = jnp.max(acc[...], axis=1)
        top = jnp.max(top, axis=1, keepdims=True)
        lane = lax.broadcasted_iota(jnp.int32, (blocks, 128), 1)
        row = lax.broadcasted_iota(jnp.int32, (blocks, 128), 0)
        flat = jnp.max(jnp.where(lane == row, top, 0.0), axis=0, keepdims=True)
        msg[...] = jnp.broadcast_to(flat, msg.shape)
        for j in range(1, dp):
            dm_copy(j).start()

    def stage_out(k):
        for j in range(1, grp):
            q_arrival(k, j).wait_recv()
        value = qbuf[k, 0].astype(jnp.float32)
        for a in range(1, grp):
            value = value + qbuf[k, a].astype(jnp.float32)
        out[k] = (value / scale_buf[k] / (dp * grp)).astype(jnp.bfloat16)

    stages = tuple(zip((stage_z, stage_q, stage_out), DELAYS))

    def tick(t, carry):
        for stage, delay in stages:
            @pl.when((t >= delay) & (t < K + delay))
            def _(stage=stage, delay=delay):
                stage(t - delay)

            if stage is stage_q:
                @pl.when(t == K - 1 + delay)
                def _():
                    stage_max()
        return carry

    lax.fori_loop(0, K + DELAYS[-1], tick, 0)

    for j in range(1, dp):
        dm_copy(j).wait_recv()
    top = msg[...]
    for j in range(1, dp):
        top = jnp.maximum(top, dpmax[j - 1])
    grpmsg[...] = top
    for j in range(1, grp):
        gm_copy(j).start()
    for j in range(1, grp):
        gm_copy(j).wait_recv()
    for j in range(1, grp):
        top = jnp.maximum(top, grpmax[j - 1])
    amax_out[...] = top.astype(jnp.bfloat16)

    def finish(k, carry):
        for j in range(1, Y):
            y_copy(k, j).wait_send()
        for j in range(1, Z):
            z_copy(k, j).wait_send()
        for j in range(1, grp):
            q_copy(k, j).wait_send()
        return carry

    lax.fori_loop(0, K, finish, 0)
    for j in range(1, dp):
        dm_copy(j).wait_send()
    for j in range(1, grp):
        gm_copy(j).wait_send()


def body(gradients, block_len, amax_history):
    dp = lax.axis_size("dp")
    grp = lax.axis_size("grp")
    rows, lanes = gradients.shape[2:]
    Y = y_extent(dp)
    Z = dp // Y
    K = min(CHUNKS, rows // dp // 32)
    lines = rows // dp // K
    piece = 32
    blocks = block_len.shape[0]
    cfg = (dp, grp, Y, Z, K, lines, piece)
    bf, f32 = jnp.bfloat16, jnp.float32
    sem = pltpu.SemaphoreType.DMA
    tile = (lines, lanes)
    scratch = [
        pltpu.VMEM((K, Z) + tile, bf),
        pltpu.VMEM((K, Y - 1, Z) + tile, bf),
        pltpu.VMEM((K, Z - 1) + tile, bf),
        pltpu.VMEM((K, Z - 1) + tile, bf),
        pltpu.VMEM((K, grp) + tile, bf),
        pltpu.VMEM((K,) + tile, f32),
        pltpu.VMEM((blocks, 8, lanes), f32),
        pltpu.VMEM((blocks, 8, lanes), f32),
        pltpu.VMEM((8, lanes), f32),
        pltpu.VMEM((dp - 1, 8, lanes), f32),
        pltpu.VMEM((8, lanes), f32),
        pltpu.VMEM((grp - 1, 8, lanes), f32),
        sem((K,)),
        sem((K, Y - 1)), sem((K, Y - 1)),
        sem((K, Z - 1)), sem((K, Z - 1)),
        sem((K, grp - 1)), sem((K, grp - 1)),
        sem((dp - 1,)), sem((dp - 1,)),
        sem((grp - 1,)), sem((grp - 1,)),
    ]
    mean, top = pl.pallas_call(
        functools.partial(kernel, cfg),
        out_shape=(
            jax.ShapeDtypeStruct((K,) + tile, bf),
            jax.ShapeDtypeStruct((8, lanes), bf),
        ),
        in_specs=[
            pl.BlockSpec(memory_space=pltpu.SMEM),
            pl.BlockSpec(memory_space=pltpu.SMEM),
            pl.BlockSpec(memory_space=pltpu.HBM),
        ],
        out_specs=(
            pl.BlockSpec(memory_space=pltpu.VMEM),
            pl.BlockSpec(memory_space=pltpu.VMEM),
        ),
        scratch_shapes=scratch,
        compiler_params=pltpu.CompilerParams(collective_id=0, has_side_effects=True),
    )(block_len, amax_history, gradients.reshape((Z, Y, K) + tile))
    return mean.reshape(rows // dp, lanes), top[0, :blocks]


def solution(mesh):
    placed = (P("grp", "dp", None, None), P(), P())
    return jax.shard_map(
        body, mesh=mesh, in_specs=placed, out_specs=(P("dp", None), P()), check_vma=False
    )
```

time: 73.8 us -> 73.3 us (level)
    squeeze x0 -> x1, local copies, waits for them, and re-layouts: none -> 1.19 us  [body(): return (mean.reshape(rows // dp, lanes), top[0, :blocks])]
where the time goes in v2:
time: 73.3 us; the launch traced here: 73.1 us
  Pallas kernels  69.4 us (95%)
  local copies, waits for them, and re-layouts  3.05 us (4%)
    pallas_call x1, Pallas kernels, body(): pl.pallas_call(functools.partial(kernel, cfg), out_shape=(jax.ShapeDtypeS...  69.4 us
    unnamed x1, local copies, waits for them, and re-layouts  1.87 us

profile of v2, /device:TPU:0, one launch (start us, length us, event | category | flops | bytes accessed | tf_op | source)
XLA Modules:
  0.0 73.1 jit_solution(17378914229364268451)
XLA Ops:
  0.6 69.4 %shard_map.50 = (bf16[16,128,128]{2,1,0:T(8,128)(2,1)}, bf16[8,128]{1,0:T(8,128)(2,1)}) custom-call(s32[16]{0:T(128)} %len_ref.1, f32[4,16]{1,0:T(4,128)} %hist_ref.1, bf16[4,2,16,128,128]{4,3,2,1,0:T(8,128)(2,1)} %bitcast.4), custom_call_target="tpu_custom_call" | custom-call | tf_op jit(solution)/shard_map/pallas_call | solution.py:251
  70.0 1.2 %slice_bitcast_fusion = bf16[16]{0:T(256)(128)(2,1)} fusion(bf16[8,128]{1,0:T(8,128)(2,1)} %get-tuple-element.5), kind=kLoop, calls=%fused_computation | loop fusion | bytes 64 | tf_op jit(solution)/shard_map/squeeze | solution.py:269
  71.2 1.9 %copy.6 = bf16[2048,128]{1,0:T(8,128)(2,1)} copy(bf16[2048,128]{1,0:T(8,128)(2,1)} %bitcast.5) | data formatting | bytes 1048576

commit v3 on v2

v3 whole, which is shorter than its diff:
```python
import functools

import jax
import jax.numpy as jnp
from jax import lax
from jax.experimental import pallas as pl
from jax.experimental.pallas import tpu as pltpu
from jax.sharding import PartitionSpec as P

SATURATE = 448.0
CHUNKS = 16
Z_FIRST = 3
STEP = 1
MESH = pl.DeviceIdType.MESH


def y_extent(dp):
    y = 1
    while (2 * y) * (2 * y) <= dp:
        y *= 2
    return y


def kernel(
    cfg, len_ref, hist_ref, grad, out, amax_out,
    own, ybuf, zin, zout, own_b, zin_b, zout_b, mout_b, yin_b,
    qbuf, scale_buf, svec, acc, msg, maxima,
    own_sem, y_send, y_recv, z_send, z_recv, q_send, q_recv,
    ob_sem, yb_send, yb_recv, zb_send, zb_recv, m_send, m_recv,
):
    dp, grp, Y, Z, K, NB, lines, piece = cfg
    NA = K - NB
    blocks = len_ref.shape[0]
    hist = hist_ref.shape[0]
    devices = dp * grp
    d = lax.axis_index("dp")
    g = lax.axis_index("grp")
    z, y = d // Y, d % Y
    base = d * (K * lines)

    def copy(src, dst, send, recv, target):
        return pltpu.make_async_remote_copy(
            src_ref=src, dst_ref=dst, send_sem=send, recv_sem=recv,
            device_id=target, device_id_type=MESH,
        )

    def own_copy(a):
        return pltpu.make_async_copy(grad.at[:, y, NB + a], own.at[a], own_sem.at[a])

    def own_b_copy(b):
        return pltpu.make_async_copy(grad.at[:, :, b], own_b.at[b], ob_sem.at[b])

    def y_copy(a, j):
        peer = (y + j) % Y
        return copy(grad.at[:, peer, NB + a], ybuf.at[a, j - 1], y_send.at[a, j - 1],
                    y_recv.at[a, j - 1], {"dp": z * Y + peer})

    def yb_copy(b, j):
        peer = (y + j) % Y
        return copy(mout_b.at[b, j - 1], yin_b.at[b, j - 1], yb_send.at[b, j - 1],
                    yb_recv.at[b, j - 1], {"dp": z * Y + peer})

    chain_a = (zin, zout, z_send, z_recv)
    chain_b = (zin_b, zout_b, zb_send, zb_recv)

    def hop(chain, i, way, t):
        into, outof, send, recv = chain
        return copy(outof.at[i, t], into.at[i, way, t], send.at[i, t], recv.at[i, way, t],
                    {"dp": (z + 1 - 2 * way) * Y + y})

    def arrival(chain, i, way, t):
        into, outof, send, recv = chain
        return copy(into.at[i, way, t], into.at[i, way, t], send.at[i, t], recv.at[i, way, t],
                    {"dp": (z - 1 + 2 * way) * Y + y})

    def await_hop(chain, i, way, t):
        @pl.when(z > 0 if way == 0 else z < Z - 1)
        def _():
            arrival(chain, i, way, t).wait_recv()

    def q_copy(k, j):
        return copy(qbuf.at[k, g], qbuf.at[k, g], q_send.at[k, j - 1], q_recv.at[k, j - 1],
                    {"grp": (g + j) % grp})

    def q_arrival(k, j):
        peer = (g + grp - j) % grp
        return copy(qbuf.at[k, peer], qbuf.at[k, peer], q_send.at[k, j - 1],
                    q_recv.at[k, j - 1], {"grp": peer})

    def device(j):
        flat = (d * grp + g + j) % devices
        return {"dp": flat // grp, "grp": flat % grp}

    def m_copy(j):
        return copy(msg, maxima.at[j - 1], m_send.at[j - 1], m_recv.at[j - 1], device(j))

    def every(action):
        def one(j, carry):
            action(j)
            return carry

        lax.fori_loop(1, devices, one, 0)

    barrier = pltpu.get_barrier_semaphore()
    every(lambda j: pl.semaphore_signal(
        barrier, inc=1, device_id=device(j), device_id_type=MESH))

    def each(count, action):
        def one(i, carry):
            action(i)
            return carry

        lax.fori_loop(0, count, one, 0)

    def upto(limit, action):
        for i in range(Z - 1):
            pl.when(limit > i)(functools.partial(action, i))

    each(NB, lambda b: own_b_copy(b).start())
    each(NA, lambda a: own_copy(a).start())
    for way, end in ((0, 0), (1, Z - 1)):
        @pl.when(z == end)
        def _(way=way):
            def clear(chain):
                into = chain[0]

                def one(i):
                    into[i, way] = jnp.zeros(into.shape[2:], into.dtype)

                return one

            each(NA, clear(chain_a))
            each(NB, clear(chain_b))
    ends = []
    total = jnp.int32(0)
    for c in range(blocks):
        total = total + len_ref[c]
        ends.append(total)
        top = jnp.full((8, 128), hist_ref[0, c], jnp.float32)
        for h in range(1, hist):
            top = jnp.maximum(top, jnp.full((8, 128), hist_ref[h, c], jnp.float32))
        svec[c] = SATURATE / jnp.maximum(top, 1.0)
    acc[...] = jnp.zeros(acc.shape, jnp.float32)
    pl.semaphore_wait(barrier, devices - 1)

    def send_y(a):
        for j in range(1, Y):
            y_copy(a, j).start()

    each(NA, send_y)

    def term_a(a, t):
        value = own[a, t].astype(jnp.float32)
        for i in range(Y - 1):
            value = value + ybuf[a, i, t].astype(jnp.float32)
        return value

    def term_b(b, t):
        return own_b[b, t].astype(jnp.float32)

    def stage_y(a):
        own_copy(a).wait()
        for j in range(1, Y):
            y_copy(a, j).wait_recv()

    def pass_on(chain, term, i, way):
        def one(s):
            t = Z - 1 - s if way == 0 else s
            await_hop(chain, i, way, t)
            value = term(i, t) + chain[0][i, way, t].astype(jnp.float32)
            chain[1][i, t] = value.astype(jnp.bfloat16)
            hop(chain, i, way, t).start()

        upto(Z - 1 - z if way == 0 else z, one)

    def merge_b(b):
        for way in range(2):
            await_hop(chain_b, b, way, z)
        for j in range(1, Y):
            peer = (y + j) % Y
            value = own_b[b, z, peer].astype(jnp.float32)
            for way in range(2):
                value = value + zin_b[b, way, z, peer].astype(jnp.float32)
            mout_b[b, j - 1] = value.astype(jnp.bfloat16)
            yb_copy(b, j).start()

    def q_a(a):
        for way in range(2):
            await_hop(chain_a, a, way, z)

        def total(rows):
            value = own[a, z, rows].astype(jnp.float32)
            for i in range(Y - 1):
                value = value + ybuf[a, i, z, rows].astype(jnp.float32)
            for way in range(2):
                value = value + zin[a, way, z, rows].astype(jnp.float32)
            return value

        stage_q(NB + a, total)

    def q_b(b):
        for j in range(1, Y):
            yb_copy(b, j).wait_recv()

        def total(rows):
            value = own_b[b, z, y, rows].astype(jnp.float32)
            for way in range(2):
                value = value + zin_b[b, way, z, y, rows].astype(jnp.float32)
            for i in range(Y - 1):
                value = value + yin_b[b, i, rows].astype(jnp.float32)
            return value

        stage_q(b, total)

    def stage_q(k, total):
        def step(i, tops):
            rows = pl.ds(pl.multiple_of(i * piece, piece), piece)
            value = total(rows)
            value = value.reshape(piece // 8, 8, 128)
            shape = value.shape
            first = (base + k * lines + i * piece) * 128
            place = (
                lax.broadcasted_iota(jnp.int32, shape, 0) * 1024
                + lax.broadcasted_iota(jnp.int32, shape, 1) * 128
                + lax.broadcasted_iota(jnp.int32, shape, 2)
            ) + first
            size = jnp.abs(value)
            scale = jnp.broadcast_to(svec[0][None], shape)
            below = place < ends[0]
            new = [jnp.maximum(tops[0], jnp.max(jnp.where(below, size, 0.0), axis=0))]
            for c in range(1, blocks):
                after = place >= ends[c - 1]
                scale = jnp.where(after, svec[c][None], scale)
                inside = after & (place < ends[c])
                new.append(jnp.maximum(tops[c], jnp.max(jnp.where(inside, size, 0.0), axis=0)))
            scale_buf[k, rows] = scale.reshape(piece, 128)
            quant = jnp.clip(value * scale, -SATURATE, SATURATE)
            qbuf[k, g, rows] = quant.reshape(piece, 128).astype(jnp.bfloat16)
            return tuple(new)

        tops = lax.fori_loop(0, lines // piece, step, tuple(acc[c] for c in range(blocks)))
        for c in range(blocks):
            acc[c] = tops[c]
        for j in range(1, grp):
            q_copy(k, j).start()

    def stage_max():
        top = jnp.max(acc[...], axis=1)
        top = jnp.max(top, axis=1, keepdims=True)
        lane = lax.broadcasted_iota(jnp.int32, (blocks, 128), 1)
        row = lax.broadcasted_iota(jnp.int32, (blocks, 128), 0)
        flat = jnp.max(jnp.where(lane == row, top, 0.0), axis=0, keepdims=True)
        msg[...] = flat
        every(lambda j: m_copy(j).start())

    def stage_out(k):
        for j in range(1, grp):
            q_arrival(k, j).wait_recv()
        value = qbuf[k, 0].astype(jnp.float32)
        for a in range(1, grp):
            value = value + qbuf[k, a].astype(jnp.float32)
        out[k] = (value / scale_buf[k] / (dp * grp)).astype(jnp.bfloat16)

    reach = STEP * (Z - 1)
    last = K + reach
    stages = (
        (lambda b: own_b_copy(b).wait(), NB, 0),
        (lambda b: pass_on(chain_b, term_b, b, 0), NB, STEP * z),
        (lambda b: pass_on(chain_b, term_b, b, 1), NB, STEP * (Z - 1 - z)),
        (merge_b, NB, reach + 1),
        (stage_y, NA, NB),
        (lambda a: pass_on(chain_a, term_a, a, 0), NA, NB + STEP * z),
        (lambda a: pass_on(chain_a, term_a, a, 1), NA, NB + STEP * (Z - 1 - z)),
        (q_b, NB, K),
        (q_a, NA, NB + reach + 1),
        (lambda b: stage_out(b), NB, K + 2),
        (lambda a: stage_out(NB + a), NA, NB + reach + 3),
    )

    def tick(t, carry):
        for stage, count, delay in stages:
            @pl.when((t >= delay) & (t < count + delay))
            def _(stage=stage, delay=delay):
                stage(t - delay)

            if stage is q_a:
                @pl.when(t == last)
                def _():
                    stage_max()
        return carry

    lax.fori_loop(0, K + reach + 3, tick, 0)

    every(lambda j: m_copy(j).wait_recv())
    top = jnp.maximum(jnp.max(maxima[...], axis=0), msg[...])
    amax_out[...] = jnp.broadcast_to(top, amax_out.shape).astype(jnp.bfloat16)

    def finish_a(a):
        for j in range(1, Y):
            y_copy(a, j).wait_send()
        upto(Z - 1 - z, lambda s: hop(chain_a, a, 0, Z - 1 - s).wait_send())
        upto(z, lambda s: hop(chain_a, a, 1, s).wait_send())

    def finish_b(b):
        for j in range(1, Y):
            yb_copy(b, j).wait_send()
        upto(Z - 1 - z, lambda s: hop(chain_b, b, 0, Z - 1 - s).wait_send())
        upto(z, lambda s: hop(chain_b, b, 1, s).wait_send())

    def finish(k):
        for j in range(1, grp):
            q_copy(k, j).wait_send()

    each(NA, finish_a)
    each(NB, finish_b)
    each(K, finish)
    every(lambda j: m_copy(j).wait_send())


def body(gradients, block_len, amax_history):
    dp = lax.axis_size("dp")
    grp = lax.axis_size("grp")
    rows, lanes = gradients.shape[2:]
    Y = y_extent(dp)
    Z = dp // Y
    K = min(CHUNKS, rows // dp // 32)
    NB = min(Z_FIRST, K - 1)
    NA = K - NB
    lines = rows // dp // K
    piece = 32
    blocks = block_len.shape[0]
    cfg = (dp, grp, Y, Z, K, NB, lines, piece)
    bf, f32 = jnp.bfloat16, jnp.float32
    sem = pltpu.SemaphoreType.DMA
    tile = (lines, lanes)
    scratch = [
        pltpu.VMEM((NA, Z) + tile, bf),
        pltpu.VMEM((NA, Y - 1, Z) + tile, bf),
        pltpu.VMEM((NA, 2, Z) + tile, bf),
        pltpu.VMEM((NA, Z) + tile, bf),
        pltpu.VMEM((NB, Z, Y) + tile, bf),
        pltpu.VMEM((NB, 2, Z, Y) + tile, bf),
        pltpu.VMEM((NB, Z, Y) + tile, bf),
        pltpu.VMEM((NB, Y - 1) + tile, bf),
        pltpu.VMEM((NB, Y - 1) + tile, bf),
        pltpu.VMEM((K, grp) + tile, bf),
        pltpu.VMEM((K,) + tile, f32),
        pltpu.VMEM((blocks, 8, lanes), f32),
        pltpu.VMEM((blocks, 8, lanes), f32),
        pltpu.VMEM((1, lanes), f32),
        pltpu.VMEM((dp * grp - 1, 1, lanes), f32),
        sem((NA,)),
        sem((NA, Y - 1)), sem((NA, Y - 1)),
        sem((NA, Z)), sem((NA, 2, Z)),
        sem((K, grp - 1)), sem((K, grp - 1)),
        sem((NB,)),
        sem((NB, Y - 1)), sem((NB, Y - 1)),
        sem((NB, Z)), sem((NB, 2, Z)),
        sem((dp * grp - 1,)), sem((dp * grp - 1,)),
    ]
    mean, top = pl.pallas_call(
        functools.partial(kernel, cfg),
        out_shape=(
            jax.ShapeDtypeStruct((K,) + tile, bf),
            jax.ShapeDtypeStruct((8, lanes), bf),
        ),
        in_specs=[
            pl.BlockSpec(memory_space=pltpu.SMEM),
            pl.BlockSpec(memory_space=pltpu.SMEM),
            pl.BlockSpec(memory_space=pltpu.HBM),
        ],
        out_specs=(
            pl.BlockSpec(memory_space=pltpu.VMEM),
            pl.BlockSpec(memory_space=pltpu.VMEM),
        ),
        scratch_shapes=scratch,
        compiler_params=pltpu.CompilerParams(collective_id=0, has_side_effects=True),
    )(block_len, amax_history, gradients.reshape((Z, Y, K) + tile))
    return mean.reshape(rows // dp, lanes), top[0, :blocks]


def solution(mesh):
    placed = (P("grp", "dp", None, None), P(), P())
    return jax.shard_map(
        body, mesh=mesh, in_specs=placed, out_specs=(P("dp", None), P()), check_vma=False
    )
```

time: 73.3 us -> 70 us (0.955)
  Pallas kernels: 69.4 us -> 66.1 us
    pallas_call x1, Pallas kernels: 69.4 us -> 66.1 us  [body(): pl.pallas_call(functools.partial(kernel, cfg), out_shape=(jax.ShapeDtypeS...]
where the time goes in v3:
time: 70 us; the launch traced here: 69.8 us
  Pallas kernels  66.1 us (94%)
  local copies, waits for them, and re-layouts  3.05 us (4%)
    pallas_call x1, Pallas kernels, body(): pl.pallas_call(functools.partial(kernel, cfg), out_shape=(jax.ShapeDtypeS...  66.1 us
    unnamed x1, local copies, waits for them, and re-layouts  1.87 us

profile of v3, /device:TPU:0, one launch (start us, length us, event | category | flops | bytes accessed | tf_op | source)
XLA Modules:
  0.0 69.8 jit_solution(17522438312435247626)
XLA Ops:
  0.6 66.1 %shard_map.50 = (bf16[16,128,128]{2,1,0:T(8,128)(2,1)}, bf16[8,128]{1,0:T(8,128)(2,1)}) custom-call(s32[16]{0:T(128)} %len_ref.1, f32[4,16]{1,0:T(4,128)} %hist_ref.1, bf16[4,2,16,128,128]{4,3,2,1,0:T(8,128)(2,1)} %bitcast.4), custom_call_target="tpu_custom_call" | custom-call | tf_op jit(solution)/shard_map/pallas_call | solution.py:361
  66.7 1.2 %slice_bitcast_fusion = bf16[16]{0:T(256)(128)(2,1)} fusion(bf16[8,128]{1,0:T(8,128)(2,1)} %get-tuple-element.5), kind=kLoop, calls=%fused_computation | loop fusion | bytes 64 | tf_op jit(solution)/shard_map/squeeze | solution.py:379
  67.9 1.9 %copy.6 = bf16[2048,128]{1,0:T(8,128)(2,1)} copy(bf16[2048,128]{1,0:T(8,128)(2,1)} %bitcast.5) | data formatting | bytes 1048576

commit v4 on v3

--- a/solution.py
+++ b/solution.py
@@ -273,8 +273,8 @@
         (lambda a: pass_on(chain_a, term_a, a, 1), NA, NB + STEP * (Z - 1 - z)),
         (q_b, NB, K),
         (q_a, NA, NB + reach + 1),
-        (lambda b: stage_out(b), NB, K + 2),
-        (lambda a: stage_out(NB + a), NA, NB + reach + 3),
+        (lambda b: stage_out(b), NB, K + 3),
+        (lambda a: stage_out(NB + a), NA, NB + reach + 4),
     )
 
     def tick(t, carry):
@@ -289,7 +289,7 @@
                     stage_max()
         return carry
 
-    lax.fori_loop(0, K + reach + 3, tick, 0)
+    lax.fori_loop(0, K + reach + 4, tick, 0)
 
     every(lambda j: m_copy(j).wait_recv())
     top = jnp.maximum(jnp.max(maxima[...], axis=0), msg[...])

time: 70 us -> 69.2 us (0.989)
  Pallas kernels: 66.1 us -> 65.3 us
    pallas_call x1, Pallas kernels: 66.1 us -> 65.3 us  [body(): pl.pallas_call(functools.partial(kernel, cfg), out_shape=(jax.ShapeDtypeS...]
where the time goes in v4:
time: 69.2 us; the launch traced here: 69 us
  Pallas kernels  65.3 us (94%)
  local copies, waits for them, and re-layouts  3.05 us (4%)
    pallas_call x1, Pallas kernels, body(): pl.pallas_call(functools.partial(kernel, cfg), out_shape=(jax.ShapeDtypeS...  65.3 us
    unnamed x1, local copies, waits for them, and re-layouts  1.87 us

profile of v4, /device:TPU:0, one launch (start us, length us, event | category | flops | bytes accessed | tf_op | source)
XLA Modules:
  0.0 69.0 jit_solution(11665397547488170121)
XLA Ops:
  0.6 65.3 %shard_map.50 = (bf16[16,128,128]{2,1,0:T(8,128)(2,1)}, bf16[8,128]{1,0:T(8,128)(2,1)}) custom-call(s32[16]{0:T(128)} %len_ref.1, f32[4,16]{1,0:T(4,128)} %hist_ref.1, bf16[4,2,16,128,128]{4,3,2,1,0:T(8,128)(2,1)} %bitcast.4), custom_call_target="tpu_custom_call" | custom-call | tf_op jit(solution)/shard_map/pallas_call | solution.py:361
  65.9 1.2 %slice_bitcast_fusion = bf16[16]{0:T(256)(128)(2,1)} fusion(bf16[8,128]{1,0:T(8,128)(2,1)} %get-tuple-element.5), kind=kLoop, calls=%fused_computation | loop fusion | bytes 64 | tf_op jit(solution)/shard_map/squeeze | solution.py:379
  67.1 1.9 %copy.6 = bf16[2048,128]{1,0:T(8,128)(2,1)} copy(bf16[2048,128]{1,0:T(8,128)(2,1)} %bitcast.5) | data formatting | bytes 1048576
